TPU v7x, 32 devices: a whole 2x2x4 slice. The times are simulated.
32 devices in a mesh: seg: 16 (over z, x, core), freq: 2 (over y).
Axes of the slice: x: 2, y: 2, z: 4, core: 2. Of those that a mesh axis runs over, the one named last changes fastest.
Arguments:
- coarse: float32 [64, 128, 2048], P('seg', None, 'freq'), may hold values from 0.5 to 8
- offsets: int32 [64, 32], replicated, may hold values from -8 to 8, as said below
Outputs:
- fine: float32 [32, 128, 2048], P(None, 'seg', 'freq')
- peaks: float32 [128], P('seg')
Inputs may be any that keep to these rules, and one draw needn't show every extreme that they name: `offsets`: every entry lies in -8 to 8, and both ends occur in every draw.
All inputs are finite; a program needn't handle non-finite values.
Results may differ from a plain program's by a relative error of at most 0.0003.
Values sent between devices are 32-bit elements; how exact they have to be, the bound alone decides.
A program may use at most 128 MiB of HBM per device.

v0:
```python
import functools

import jax
import jax.numpy as jnp
from jax import lax
from jax.experimental import pallas as pl
from jax.experimental.pallas import tpu as pltpu
from jax.sharding import PartitionSpec as P

HALO = 8
EDGE = 128
SHIFTS = 2 * HALO + 1
MESH = pl.DeviceIdType.MESH


def partner(me, step, count):
    if count & (count - 1):
        return lax.rem(step + count - me, count)
    result = me
    bit = 1
    while bit < count:
        wanted = (step // bit) % 2 if isinstance(step, int) else lax.rem(step // bit, 2)
        held = lax.rem(me // bit, 2)
        result = result + bit * wanted * (1 - 2 * held)
        bit *= 2
    return result


def kernel(
    nseg,
    nfreq,
    coarse,
    offsets,
    total,
    peaks,
    maps,
    low,
    high,
    shifted,
    tops,
    shifts,
    own_sem,
    shifts_sem,
    edge_sem,
    edge_recv,
    send_sem,
    recv_sem,
    up_send,
    up_recv,
    down_send,
    down_recv,
    top_send,
    top_recv,
):
    local_segs = coarse.shape[0]
    spins, rows, bins = total.shape
    parts = recv_sem.shape[0]
    part_segs = local_segs // parts
    scale = 1.0 / (nseg * local_segs)
    me = lax.axis_index("seg")
    band = lax.axis_index("freq")

    def mine(target):
        return coarse.at[:, pl.ds(pl.multiple_of(target * rows, rows), rows), :]

    early = EDGE if nfreq == 2 else bins
    edge_at = jnp.where(band == 0, bins - early, 0)
    rest_at = jnp.where(band == 0, 0, early)

    def piece(step, begin, size, segs, sent, received):
        other = partner(me, step, nseg)
        columns = pl.ds(pl.multiple_of(begin, EDGE), size)
        rows_of = pl.ds(pl.multiple_of(other * rows, rows), rows)
        return pltpu.make_async_remote_copy(
            src_ref=coarse.at[segs, rows_of, columns],
            dst_ref=maps.at[step, segs, :, columns],
            send_sem=sent,
            recv_sem=received,
            device_id={"seg": other, "freq": band},
            device_id_type=MESH,
        )

    def edge(step):
        return piece(step, edge_at, early, pl.ds(0, local_segs), edge_sem.at[step], edge_recv.at[step])

    def rest(step, part):
        segs = pl.ds(part * part_segs, part_segs)
        return piece(step, rest_at, bins - early, segs, send_sem.at[part, step], recv_sem.at[part, step])

    def upward(step):
        return pltpu.make_async_remote_copy(
            src_ref=maps.at[step, :, :, pl.ds(bins - EDGE, EDGE)],
            dst_ref=low.at[step],
            send_sem=up_send.at[step],
            recv_sem=up_recv.at[step],
            device_id={"seg": me, "freq": band + 1},
            device_id_type=MESH,
        )

    def downward(step):
        return pltpu.make_async_remote_copy(
            src_ref=maps.at[step, :, :, pl.ds(0, EDGE)],
            dst_ref=high.at[step],
            send_sem=down_send.at[step],
            recv_sem=down_recv.at[step],
            device_id={"seg": me, "freq": band - 1},
            device_id_type=MESH,
        )

    own = pltpu.make_async_copy(mine(me), maps.at[0], own_sem)
    own.start()

    barrier = pltpu.get_barrier_semaphore()

    for step in reversed(range(1, nseg)):
        pl.semaphore_signal(
            barrier, inc=1, device_id={"seg": partner(me, step, nseg), "freq": band}, device_id_type=MESH
        )

    for step in range(1, nfreq):
        pl.semaphore_signal(
            barrier, inc=1, device_id={"seg": me, "freq": lax.rem(band + step, nfreq)}, device_id_type=MESH
        )

    load_shifts = pltpu.make_async_copy(offsets, shifts, shifts_sem)
    load_shifts.start()
    total[...] = jnp.zeros_like(total)

    @pl.when(band == 0)
    def _():
        low[...] = jnp.zeros_like(low)

    @pl.when(band == nfreq - 1)
    def _():
        high[...] = jnp.zeros_like(high)

    pl.semaphore_wait(barrier, nseg - 1 + nfreq - 1)

    @pl.loop(1, nseg)
    def _(step):
        edge(step).start()

    if early < bins:

        @pl.loop(1, nseg)
        def _(step):
            for part in range(parts):
                rest(step, part).start()

    def forward(step):
        @pl.when(band < nfreq - 1)
        def _():
            upward(step).start()

        @pl.when(band > 0)
        def _():
            downward(step).start()

    def wait_edges(step):
        @pl.when(band < nfreq - 1)
        def _():
            downward(step).wait_recv()

        @pl.when(band > 0)
        def _():
            upward(step).wait_recv()

    def add(step, part, best=None):
        first = partner(me, step, nseg) * local_segs
        segs = range(part * part_segs, (part + 1) * part_segs)
        lane = lax.broadcasted_iota(jnp.int32, (rows, EDGE), 1)
        for seg in segs:
            ring = jnp.where(lane < EDGE // 2, high[step, seg], low[step, seg])
            line = jnp.concatenate([maps[step, seg], ring], axis=1)
            width = bins + EDGE
            for shift in range(-HALO, HALO + 1):
                turned = line if shift == 0 else pltpu.roll(line, (-shift) % width, 1)
                shifted[seg, HALO + shift] = turned[:, :bins]

        def spindown(spin, best):
            value = total[spin]
            for seg in segs:
                value = value + shifted[seg, HALO + shifts[spin, first + seg]]
            if best is not None:
                value = value * scale
                best = jnp.maximum(best, value)
            total[spin] = value
            return best

        return lax.fori_loop(0, spins, spindown, best, unroll=4)

    own.wait()
    forward(0)

    @pl.loop(1, nseg)
    def _(step):
        edge(step).wait_recv()
        forward(step)

    load_shifts.wait()
    wait_edges(0)
    for part in range(parts):
        add(0, part)

    def receive(step, best=None):
        wait_edges(step)
        for part in range(parts):
            if early < bins:
                rest(step, part).wait_recv()
            last = best if part == parts - 1 else None
            result = add(step, part, last)
        return result

    @pl.loop(1, nseg - 1)
    def _(step):
        receive(step)

    best = receive(nseg - 1, jnp.full((rows, bins), -jnp.inf, jnp.float32))
    top = best[:, :EDGE]
    for begin in range(EDGE, bins, EDGE):
        top = jnp.maximum(top, best[:, begin : begin + EDGE])
    tops[0] = top

    def tell(step):
        return pltpu.make_async_remote_copy(
            src_ref=tops.at[0],
            dst_ref=tops.at[step],
            send_sem=top_send.at[step],
            recv_sem=top_recv.at[step],
            device_id={"seg": me, "freq": lax.rem(band + step, nfreq)},
            device_id_type=MESH,
        )

    for step in range(1, nfreq):
        tell(step).start()

    @pl.loop(1, nseg)
    def _(step):
        edge(step).wait_send()
        if early < bins:
            for part in range(parts):
                rest(step, part).wait_send()

    @pl.loop(0, nseg)
    def _(step):
        @pl.when(band < nfreq - 1)
        def _():
            upward(step).wait_send()

        @pl.when(band > 0)
        def _():
            downward(step).wait_send()

    for step in range(1, nfreq):
        tell(step).wait()
    peak = tops[0]
    for step in range(1, nfreq):
        peak = jnp.maximum(peak, tops[step])
    peaks[...] = peak


def finish(total, tops, fine, peaks, sem):
    write = pltpu.make_async_copy(total, fine, sem)
    write.start()
    rows, width = tops.shape
    row = lax.broadcasted_iota(jnp.int32, (rows, width), 0)
    lane = lax.broadcasted_iota(jnp.int32, (rows, width), 1)
    top = jnp.max(tops[...], axis=1, keepdims=True)
    line = jnp.sum(jnp.where(row == lane, top, 0.0), axis=0)
    peaks[...] = line[:rows]
    write.wait()


def solution(mesh):
    nseg, nfreq = mesh.shape["seg"], mesh.shape["freq"]

    def on_device(coarse, offsets):
        local_segs, points, bins = coarse.shape
        rows = points // nseg
        spins = offsets.shape[1]
        parts = 1
        total, peaks = pl.pallas_call(
            functools.partial(kernel, nseg, nfreq),
            out_shape=(
                jax.ShapeDtypeStruct((spins, rows, bins), jnp.float32),
                jax.ShapeDtypeStruct((rows, EDGE), jnp.float32),
            ),
            in_specs=[
                pl.BlockSpec(memory_space=pltpu.HBM),
                pl.BlockSpec(memory_space=pltpu.HBM),
            ],
            out_specs=(
                pl.BlockSpec(memory_space=pltpu.VMEM),
                pl.BlockSpec(memory_space=pltpu.VMEM),
            ),
            scratch_shapes=[
                pltpu.VMEM((nseg, local_segs, rows, bins), jnp.float32),
                pltpu.VMEM((nseg, local_segs, rows, EDGE), jnp.float32),
                pltpu.VMEM((nseg, local_segs, rows, EDGE), jnp.float32),
                pltpu.VMEM((local_segs, SHIFTS, rows, bins), jnp.float32),
                pltpu.VMEM((nfreq, rows, EDGE), jnp.float32),
                pltpu.SMEM(offsets.shape[::-1], jnp.int32),
                pltpu.SemaphoreType.DMA,
                pltpu.SemaphoreType.DMA,
                pltpu.SemaphoreType.DMA((nseg,)),
                pltpu.SemaphoreType.DMA((nseg,)),
                pltpu.SemaphoreType.DMA((parts, nseg)),
                pltpu.SemaphoreType.DMA((parts, nseg)),
                pltpu.SemaphoreType.DMA((nseg,)),
                pltpu.SemaphoreType.DMA((nseg,)),
                pltpu.SemaphoreType.DMA((nseg,)),
                pltpu.SemaphoreType.DMA((nseg,)),
                pltpu.SemaphoreType.DMA((nfreq,)),
                pltpu.SemaphoreType.DMA((nfreq,)),
            ],
            compiler_params=pltpu.CompilerParams(
                collective_id=0, has_side_effects=True, vmem_limit_bytes=32 << 20
            ),
        )(pltpu.with_memory_space_constraint(coarse, pltpu.HBM), pltpu.with_memory_space_constraint(offsets.T, pltpu.HBM))
        return pl.pallas_call(
            finish,
            out_shape=(
                jax.ShapeDtypeStruct((spins, rows, bins), jnp.float32),
                jax.ShapeDtypeStruct((rows,), jnp.float32),
            ),
            in_specs=[pl.BlockSpec(memory_space=pltpu.VMEM), pl.BlockSpec(memory_space=pltpu.VMEM)],
            out_specs=(pl.BlockSpec(memory_space=pltpu.HBM), pl.BlockSpec(memory_space=pltpu.VMEM)),
            scratch_shapes=[pltpu.SemaphoreType.DMA],
            compiler_params=pltpu.CompilerParams(vmem_limit_bytes=8 << 20),
        )(total, peaks)

    return jax.shard_map(
        on_device,
        mesh=mesh,
        in_specs=(P("seg", None, "freq"), P()),
        out_specs=(P(None, "seg", "freq"), P("seg")),
        check_vma=False,
    )
```

profile of v0, /device:TPU:8, one launch (start us, length us, event | category | flops | bytes accessed | tf_op | source)
XLA Modules:
  0.0 57.2 jit_solution(15190645550577688792)
XLA Ops:
  0.6 55.1 %shard_map.41 = (f32[32,8,1024]{2,1,0:T(8,128)S(1)}, f32[8,128]{1,0:T(8,128)S(1)}) custom-call(f32[4,128,1024]{2,1,0:T(8,128)} %coarse.1, s32[32,64]{1,0:T(8,128)} %bitcast.1), custom_call_target="tpu_custom_call" | custom-call | tf_op jit(solution)/shard_map/pallas_call | solution.py:282
  55.7 1.5 %shard_map.42 = (f32[32,8,1024]{2,1,0:T(8,128)}, f32[8]{0:T(128)}) custom-call(f32[32,8,1024]{2,1,0:T(8,128)S(1)} %get-tuple-element.4.total, f32[8,128]{1,0:T(8,128)S(1)} %get-tuple-element.5.tops), custom_call_target="tpu_custom_call" | custom-call | tf_op jit(solution)/shard_map/pallas_call | solution.py:320
where the time goes:
time: 57.3 us; the launch traced here: 57.2 us
  Pallas kernels  56.6 us (99%)
  between operations  0.64 us (1%)
    pallas_call x1, Pallas kernels, on_device(): pl.pallas_call(functools.partial(kernel, nseg, nfreq), out_shape=(jax.Sha...  55.1 us
    pallas_call x1, Pallas kernels, on_device(): pl.pallas_call(finish, out_shape=(jax.ShapeDtypeStruct((spins, rows, bins...  1.49 us

commit v1 on v0

v1 whole, which is shorter than its diff:
```python
import functools

import jax
import jax.numpy as jnp
from jax import lax
from jax.experimental import pallas as pl
from jax.experimental.pallas import tpu as pltpu
from jax.sharding import PartitionSpec as P

HALO = 8
EDGE = 128
SHIFTS = 2 * HALO + 1
PLANES = 4
LEAD = 2
MESH = pl.DeviceIdType.MESH


def partner(me, step, count):
    result = me
    bit = 1
    while bit < count:
        wanted = (step // bit) % 2 if isinstance(step, int) else lax.rem(step // bit, 2)
        held = lax.rem(me // bit, 2)
        result = result + bit * wanted * (1 - 2 * held)
        bit *= 2
    return result


def kernel(
    nseg,
    nfreq,
    tail,
    coarse,
    offsets,
    total,
    tops,
    maps,
    low,
    high,
    shifted,
    shifts,
    own_sem,
    shifts_sem,
    send_sem,
    edge_recv,
    bulk_recv,
    tail_recv,
    up_send,
    up_recv,
    down_send,
    down_recv,
    top_send,
    top_recv,
    near_sem,
    far_sem,
):
    local_segs = coarse.shape[0]
    spins, rows, bins = total.shape
    scale = 1.0 / (nseg * local_segs)
    size = nseg // PLANES
    bulk = local_segs - tail
    me = lax.axis_index("seg")
    band = lax.axis_index("freq")
    plane = me // size
    inner = lax.rem((plane + 1) // 2, 2) == 1
    outer = jnp.logical_not(inner)

    early = EDGE if nfreq <= 2 else bins
    edge_at = jnp.where(band == 0, bins - early, 0)
    rest_at = jnp.where(band == 0, 0, early)

    def each(group, begin, end, act):
        @pl.loop(begin, end)
        def _(j):
            act(group * size + j)

    def greet(step, sem):
        pl.semaphore_signal(
            sem, inc=1, device_id={"seg": partner(me, step, nseg), "freq": band}, device_id_type=MESH
        )

    def greet_bands(sem):
        for step in range(1, nfreq):
            pl.semaphore_signal(
                sem, inc=1, device_id={"seg": me, "freq": lax.rem(band + step, nfreq)}, device_id_type=MESH
            )

    def piece(step, begin, width, segs, received):
        other = partner(me, step, nseg)
        columns = pl.ds(pl.multiple_of(begin, EDGE), width)
        rows_of = pl.ds(pl.multiple_of(other * rows, rows), rows)
        return pltpu.make_async_remote_copy(
            src_ref=coarse.at[segs, rows_of, columns],
            dst_ref=maps.at[step, segs, :, columns],
            send_sem=send_sem,
            recv_sem=received,
            device_id={"seg": other, "freq": band},
            device_id_type=MESH,
        )

    def send_edge(step):
        piece(step, edge_at, early, pl.ds(0, local_segs), edge_recv.at[step // size]).start()

    def bulk_of(step):
        return piece(step, rest_at, bins - early, pl.ds(0, bulk), bulk_recv.at[step])

    def tail_of(step):
        return piece(step, rest_at, bins - early, pl.ds(bulk, tail), tail_recv.at[step])

    def send_bulk(step):
        if early < bins:
            bulk_of(step).start()

    def send_tail(step):
        if early < bins:
            tail_of(step).start()

    def wait_edges(group, first):
        there = maps.at[pl.ds(group * size + first, size - first), :, :, pl.ds(0, early)]
        pltpu.make_async_copy(there, there, edge_recv.at[group]).wait()

    def upward(group):
        members = pl.ds(group * size, size)
        return pltpu.make_async_remote_copy(
            src_ref=maps.at[members, :, :, pl.ds(bins - EDGE, EDGE)],
            dst_ref=low.at[members],
            send_sem=up_send,
            recv_sem=up_recv.at[group],
            device_id={"seg": me, "freq": band + 1},
            device_id_type=MESH,
        )

    def downward(group):
        members = pl.ds(group * size, size)
        return pltpu.make_async_remote_copy(
            src_ref=maps.at[members, :, :, pl.ds(0, EDGE)],
            dst_ref=high.at[members],
            send_sem=down_send,
            recv_sem=down_recv.at[group],
            device_id={"seg": me, "freq": band - 1},
            device_id_type=MESH,
        )

    def forward(group):
        @pl.when(band < nfreq - 1)
        def _():
            upward(group).start()

        @pl.when(band > 0)
        def _():
            downward(group).start()

    def wait_halo(group):
        @pl.when(band < nfreq - 1)
        def _():
            downward(group).wait_recv()

        @pl.when(band > 0)
        def _():
            upward(group).wait_recv()

    barrier = pltpu.get_barrier_semaphore()

    @pl.when(inner)
    def _():
        each(3, 0, size, lambda step: greet(step, barrier))
        each(1, 0, size, lambda step: greet(step, barrier))
        pl.semaphore_wait(barrier, size)

    @pl.when(outer)
    def _():
        greet_bands(barrier)
        pl.semaphore_wait(barrier, size + nfreq - 1)
        greet_bands(near_sem)

    first_group = jnp.where(inner, 3, 1)
    lead = min(LEAD, size)
    each(first_group, 0, size, send_edge)
    each(first_group, 0, lead, send_bulk)

    own = pltpu.make_async_copy(
        coarse.at[:, pl.ds(pl.multiple_of(me * rows, rows), rows), :], maps.at[0], own_sem
    )
    own.start()
    load_shifts = pltpu.make_async_copy(offsets, shifts, shifts_sem)
    load_shifts.start()

    @pl.when(outer)
    def _():
        if nfreq > 1:
            pl.semaphore_wait(near_sem, nfreq - 1)
        each(1, 0, size, lambda step: greet(step, near_sem))
        pl.semaphore_wait(near_sem, 1)

    @pl.when(inner)
    def _():
        pl.semaphore_wait(near_sem, size)
        greet(3 * size, far_sem)
        pl.semaphore_wait(far_sem, 1)
        greet(size, near_sem)

    each(2, 0, size, send_edge)
    each(4 - first_group, 0, size, send_edge)
    each(0, 1, size, send_edge)

    @pl.when(inner)
    def _():
        each(1, 0, size, send_bulk)
        each(1, 0, size, send_tail)
        each(0, 1, size, send_bulk)
        each(0, 1, size, send_tail)
        each(3, lead, size, send_bulk)
        each(2, 0, size, send_bulk)
        each(2, 0, size, send_tail)
        each(3, 0, size, send_tail)

    @pl.when(outer)
    def _():
        each(1, lead, size, send_bulk)
        each(1, 0, size, send_tail)
        each(0, 1, size, send_bulk)
        each(0, 1, size, send_tail)
        each(2, 0, size, send_bulk)
        each(3, 0, size, send_bulk)
        each(3, 0, size, send_tail)
        each(2, 0, size, send_tail)

    total[...] = jnp.zeros_like(total)

    @pl.when(band == 0)
    def _():
        low[...] = jnp.zeros_like(low)

    @pl.when(band == nfreq - 1)
    def _():
        high[...] = jnp.zeros_like(high)

    def add(step, begin, count, best=None):
        first = partner(me, step, nseg) * local_segs
        segs = range(begin, begin + count)
        lane = lax.broadcasted_iota(jnp.int32, (rows, EDGE), 1)
        for seg in segs:
            ring = jnp.where(lane < EDGE // 2, high[step, seg], low[step, seg])
            line = jnp.concatenate([maps[step, seg], ring], axis=1)
            width = bins + EDGE
            for shift in range(-HALO, HALO + 1):
                turned = line if shift == 0 else pltpu.roll(line, (-shift) % width, 1)
                shifted[seg, HALO + shift] = turned[:, :bins]

        def spindown(spin, best):
            value = total[spin]
            for seg in segs:
                value = value + shifted[seg, HALO + shifts[spin, first + seg]]
            if best is not None:
                value = value * scale
                best = jnp.maximum(best, value)
            total[spin] = value
            return best

        return lax.fori_loop(0, spins, spindown, best, unroll=4)

    wait_edges(first_group, 0)
    forward(first_group)
    own.wait()
    wait_edges(0, 1)
    forward(0)
    wait_edges(4 - first_group, 0)
    forward(4 - first_group)
    wait_edges(2, 0)
    forward(2)
    load_shifts.wait()

    @pl.loop(0, nseg)
    def _(turn):
        place = turn // size
        group = jnp.where(jnp.logical_and(inner, place >= 2), 5 - place, place)
        member = lax.rem(turn, size)
        step = group * size + member

        @pl.when(member == 0)
        def _():
            wait_halo(group)

        @pl.when(step > 0)
        def _():
            if early < bins:
                bulk_of(step).wait_recv()

        add(step, 0, bulk)

    def last_part(turn, best=None):
        across = turn - 2 * size
        far = (2 + lax.rem(across, 2)) * size + across // 2
        step = jnp.where(turn < 2 * size, turn, far)

        @pl.when(step > 0)
        def _():
            if early < bins:
                tail_of(step).wait_recv()

        return add(step, bulk, tail, best)

    @pl.loop(0, nseg - 1)
    def _(turn):
        last_part(turn)

    best = last_part(
        jnp.int32(nseg - 1), jnp.full((rows, bins), -jnp.inf, jnp.float32)
    )
    top = best[:, :EDGE]
    for begin in range(EDGE, bins, EDGE):
        top = jnp.maximum(top, best[:, begin : begin + EDGE])
    tops[0] = top

    def tell(step):
        return pltpu.make_async_remote_copy(
            src_ref=tops.at[0],
            dst_ref=tops.at[step],
            send_sem=top_send.at[step],
            recv_sem=top_recv.at[step],
            device_id={"seg": me, "freq": lax.rem(band + step, nfreq)},
            device_id_type=MESH,
        )

    for step in range(1, nfreq):
        tell(step).start()

    sent = coarse.at[:, pl.ds(0, (nseg - 1) * rows), :]
    pltpu.make_async_copy(sent, sent, send_sem).wait()

    @pl.when(band < nfreq - 1)
    def _():
        pltpu.make_async_copy(low, low, up_send).wait()

    @pl.when(band > 0)
    def _():
        pltpu.make_async_copy(high, high, down_send).wait()

    for step in range(1, nfreq):
        tell(step).wait()


def finish(total, tops, fine, peaks, line, sem, line_sem):
    write = pltpu.make_async_copy(total, fine, sem)
    write.start()
    bands, rows, width = tops.shape
    row = lax.broadcasted_iota(jnp.int32, (rows, width), 0)
    lane = lax.broadcasted_iota(jnp.int32, (rows, width), 1)
    top = tops[0]
    for band in range(1, bands):
        top = jnp.maximum(top, tops[band])
    top = jnp.max(top, axis=1, keepdims=True)
    line[...] = jnp.sum(jnp.where(row == lane, top, 0.0), axis=0)[:rows]
    write_line = pltpu.make_async_copy(line, peaks, line_sem)
    write_line.start()
    write.wait()
    write_line.wait()


def solution(mesh):
    nseg, nfreq = mesh.shape["seg"], mesh.shape["freq"]

    def on_device(coarse, offsets):
        local_segs, points, bins = coarse.shape
        rows = points // nseg
        spins = offsets.shape[1]
        tail = 1
        hbm = pl.BlockSpec(memory_space=pltpu.HBM)
        vmem = pl.BlockSpec(memory_space=pltpu.VMEM)
        dma = pltpu.SemaphoreType.DMA
        total, tops = pl.pallas_call(
            functools.partial(kernel, nseg, nfreq, tail),
            out_shape=(
                jax.ShapeDtypeStruct((spins, rows, bins), jnp.float32),
                jax.ShapeDtypeStruct((nfreq, rows, EDGE), jnp.float32),
            ),
            in_specs=[hbm, hbm],
            out_specs=(vmem, vmem),
            scratch_shapes=[
                pltpu.VMEM((nseg, local_segs, rows, bins), jnp.float32),
                pltpu.VMEM((nseg, local_segs, rows, EDGE), jnp.float32),
                pltpu.VMEM((nseg, local_segs, rows, EDGE), jnp.float32),
                pltpu.VMEM((local_segs, SHIFTS, rows, bins), jnp.float32),
                pltpu.SMEM(offsets.shape[::-1], jnp.int32),
                dma,
                dma,
                dma,
                dma((PLANES,)),
                dma((nseg,)),
                dma((nseg,)),
                dma,
                dma((PLANES,)),
                dma,
                dma((PLANES,)),
                dma((nfreq,)),
                dma((nfreq,)),
                pltpu.SemaphoreType.REGULAR,
                pltpu.SemaphoreType.REGULAR,
            ],
            compiler_params=pltpu.CompilerParams(
                collective_id=0, has_side_effects=True, vmem_limit_bytes=32 << 20
            ),
        )(pltpu.with_memory_space_constraint(coarse, pltpu.HBM), pltpu.with_memory_space_constraint(offsets.T, pltpu.HBM))
        return pl.pallas_call(
            finish,
            out_shape=(
                jax.ShapeDtypeStruct((spins, rows, bins), jnp.float32),
                jax.ShapeDtypeStruct((rows,), jnp.float32),
            ),
            in_specs=[vmem, vmem],
            out_specs=(hbm, hbm),
            scratch_shapes=[pltpu.VMEM((rows,), jnp.float32), dma, dma],
            compiler_params=pltpu.CompilerParams(vmem_limit_bytes=8 << 20),
        )(total, tops)

    return jax.shard_map(
        on_device,
        mesh=mesh,
        in_specs=(P("seg", None, "freq"), P()),
        out_specs=(P(None, "seg", "freq"), P("seg")),
        check_vma=False,
    )
```

time: 57.3 us -> 63.6 us (1.11)
  the two profiles are of different devices: /device:TPU:8 before, /device:TPU:0 now
where the time goes in v1:
time: 63.6 us; the launch traced here: 63.5 us
  Pallas kernels  62.8 us (99%)
  between operations  0.64 us (1%)
    pallas_call x1, Pallas kernels, on_device(): pl.pallas_call(functools.partial(kernel, nseg, nfreq, tail), out_shape=(j...  61.8 us

profile of v1, /device:TPU:0, one launch (start us, length us, event | category | flops | bytes accessed | tf_op | source)
XLA Modules:
  0.0 63.5 jit_solution(6880938632380120133)
XLA Ops:
  0.6 61.8 %shard_map.41 = (f32[32,8,1024]{2,1,0:T(8,128)S(1)}, f32[2,8,128]{2,1,0:T(8,128)S(1)}) custom-call(f32[4,128,1024]{2,1,0:T(8,128)} %coarse.1, s32[32,64]{1,0:T(8,128)} %bitcast.1), custom_call_target="tpu_custom_call" | custom-call | tf_op jit(solution)/shard_map/pallas_call | solution.py:371
  62.5 1.0 %shard_map.42 = (f32[32,8,1024]{2,1,0:T(8,128)}, f32[8]{0:T(128)}) custom-call(f32[32,8,1024]{2,1,0:T(8,128)S(1)} %get-tuple-element.4.total, f32[2,8,128]{2,1,0:T(8,128)S(1)} %get-tuple-element.5.tops), custom_call_target="tpu_custom_call" | custom-call | tf_op jit(solution)/shard_map/pallas_call | solution.py:404

commit v2 on v1

v2 whole, which is shorter than its diff:
```python
import functools

import jax
import jax.numpy as jnp
from jax import lax
from jax.experimental import pallas as pl
from jax.experimental.pallas import tpu as pltpu
from jax.sharding import PartitionSpec as P

HALO = 8
EDGE = 128
SHIFTS = 2 * HALO + 1
PLANES = 4
PAIR = 2
MESH = pl.DeviceIdType.MESH


def partner(me, step, count):
    result = me
    bit = 1
    while bit < count:
        wanted = (step // bit) % 2 if isinstance(step, int) else lax.rem(step // bit, 2)
        held = lax.rem(me // bit, 2)
        result = result + bit * wanted * (1 - 2 * held)
        bit *= 2
    return result


def kernel(
    nseg,
    nfreq,
    parts,
    coarse,
    offsets,
    total,
    maps,
    low,
    high,
    shifted,
    tops,
    shifts,
    own_sem,
    shifts_sem,
    send_sem,
    edge_recv,
    pair_recv,
    part_recv,
    halo_send,
    halo_recv,
    top_send,
    top_recv,
    near_sem,
    far_sem,
    band_sem,
):
    local_segs = coarse.shape[0]
    spins = total.shape[0] - 1
    rows, bins = total.shape[1:]
    scale = 1.0 / (nseg * local_segs)
    size = nseg // PLANES
    begins = [sum(parts[:place]) for place in range(len(parts))]
    me = lax.axis_index("seg")
    band = lax.axis_index("freq")
    plane = me // size
    inner = lax.rem((plane + 1) // 2, 2) == 1
    outer = jnp.logical_not(inner)
    last_group = jnp.where(inner, 3, 2)
    last = (last_group + 1) * size - PAIR

    early = EDGE if nfreq <= 2 else bins
    width = bins - early
    edge_at = jnp.where(band == 0, bins - early, 0)
    rest_at = jnp.where(band == 0, 0, early)

    def each(begin, end, act):
        @pl.loop(begin, end)
        def _(step):
            act(step)

    def greet(step, sem):
        pl.semaphore_signal(
            sem, inc=1, device_id={"seg": partner(me, step, nseg), "freq": band}, device_id_type=MESH
        )

    def greet_bands(sem):
        for step in range(1, nfreq):
            pl.semaphore_signal(
                sem, inc=1, device_id={"seg": me, "freq": lax.rem(band + step, nfreq)}, device_id_type=MESH
            )

    def send(step, begin, count, first, segs, received):
        other = partner(me, step, nseg)
        columns = pl.ds(pl.multiple_of(begin, EDGE), count)
        rows_of = pl.ds(pl.multiple_of(other * rows, rows), rows)
        members = pl.ds(first, segs)
        pltpu.make_async_remote_copy(
            src_ref=coarse.at[members, rows_of, columns],
            dst_ref=maps.at[step, members, :, columns],
            send_sem=send_sem,
            recv_sem=received,
            device_id={"seg": other, "freq": band},
            device_id_type=MESH,
        ).start()

    def send_edge(step):
        send(step, edge_at, early, 0, local_segs, edge_recv.at[step // size])

    def send_rest(step):
        if width:
            send(step, rest_at, width, 0, local_segs, pair_recv.at[step // PAIR])

    def part_sem(pair, place):
        return part_recv.at[place - 1] if place else pair_recv.at[pair]

    def send_parts(group):
        core = lax.rem(me, PAIR)
        first = (group + 1) * size - PAIR
        if width:
            for place, segs in enumerate(parts):
                for turn in range(PAIR):
                    step = first + lax.rem(core + turn, PAIR)
                    send(step, rest_at, width, begins[place], segs, part_sem(first // PAIR, place))

    def wait_for(there, sem):
        pltpu.make_async_copy(there, there, sem).wait()

    def wait_edges(group, first):
        wait_for(maps.at[pl.ds(group * size + first, size - first), :, :, pl.ds(0, early)], edge_recv.at[group])

    def wait_rest(step, steps, segs, sem):
        if width:
            wait_for(maps.at[pl.ds(step, steps), pl.ds(0, segs), :, pl.ds(0, width)], sem)

    def upward(group):
        members = pl.ds(group * size, size)
        return pltpu.make_async_remote_copy(
            src_ref=maps.at[members, :, :, pl.ds(bins - EDGE, EDGE)],
            dst_ref=low.at[members],
            send_sem=halo_send.at[0],
            recv_sem=halo_recv.at[0, group],
            device_id={"seg": me, "freq": band + 1},
            device_id_type=MESH,
        )

    def downward(group):
        members = pl.ds(group * size, size)
        way = halo_send.shape[0] - 1
        return pltpu.make_async_remote_copy(
            src_ref=maps.at[members, :, :, pl.ds(0, EDGE)],
            dst_ref=high.at[members],
            send_sem=halo_send.at[way],
            recv_sem=halo_recv.at[way, group],
            device_id={"seg": me, "freq": band - 1},
            device_id_type=MESH,
        )

    def forward(group):
        @pl.when(band < nfreq - 1)
        def _():
            upward(group).start()

        @pl.when(band > 0)
        def _():
            downward(group).start()

    def wait_halo(group):
        @pl.when(band < nfreq - 1)
        def _():
            downward(group).wait_recv()

        @pl.when(band > 0)
        def _():
            upward(group).wait_recv()

    barrier = pltpu.get_barrier_semaphore()

    @pl.when(inner)
    def _():
        for step in range(3 * size, 3 * size + PAIR):
            greet(step, barrier)
        for step in range(size, 2 * size):
            greet(step, barrier)
        pl.semaphore_wait(barrier, PAIR)
        for step in range(3 * size, 3 * size + PAIR):
            send_edge(step)
        for step in range(3 * size, 3 * size + PAIR):
            send_rest(step)

    @pl.when(outer)
    def _():
        greet_bands(barrier)
        pl.semaphore_wait(barrier, size + nfreq - 1)
        each(size, 2 * size, lambda step: greet(step, near_sem))
        greet_bands(band_sem)
        each(size, 2 * size, send_edge)
        each(size, size + PAIR, send_rest)

    own = pltpu.make_async_copy(
        coarse.at[:, pl.ds(pl.multiple_of(me * rows, rows), rows), :], maps.at[0], own_sem
    )
    own.start()
    load_shifts = pltpu.make_async_copy(offsets, shifts, shifts_sem)
    load_shifts.start()
    total[...] = jnp.zeros_like(total)

    @pl.when(band == 0)
    def _():
        low[...] = jnp.zeros_like(low)

    @pl.when(band == nfreq - 1)
    def _():
        high[...] = jnp.zeros_like(high)

    @pl.when(inner)
    def _():
        pl.semaphore_wait(near_sem, size)
        greet(3 * size, far_sem)
        each(size, 2 * size, send_edge)
        each(1, size, send_edge)
        each(1, 2 * size, send_rest)
        pl.semaphore_wait(far_sem, 1)
        greet(size, near_sem)
        each(3 * size + PAIR, nseg, send_edge)
        each(2 * size, 3 * size, send_edge)
        each(2 * size, 3 * size - PAIR, send_rest)
        send_parts(2)
        each(3 * size + PAIR, 4 * size - PAIR, send_rest)
        send_parts(3)
        if nfreq > 1:
            pl.semaphore_wait(band_sem, 1)

    @pl.when(outer)
    def _():
        if nfreq > 1:
            pl.semaphore_wait(band_sem, nfreq - 1)
            greet(size, band_sem)
        pl.semaphore_wait(near_sem, 1)
        each(2 * size, nseg, send_edge)
        each(1, size, send_edge)
        each(1, size, send_rest)
        each(size + PAIR, nseg, send_rest)

    def add(lines, best=None):
        lane = lax.broadcasted_iota(jnp.int32, (rows, EDGE), 1)
        columns = []
        for slot, (step, seg) in enumerate(lines):
            columns.append(partner(me, step, nseg) * local_segs + seg)
            ring = jnp.where(lane < EDGE // 2, high[step, seg], low[step, seg])
            line = jnp.concatenate([maps[step, seg], ring], axis=1)
            for shift in range(-HALO, HALO + 1):
                turned = line if shift == 0 else pltpu.roll(line, (-shift) % (bins + EDGE), 1)
                shifted[slot, HALO + shift] = turned[:, :bins]

        def spindown(spin, best):
            value = total[spin]
            for slot, column in enumerate(columns):
                value = value + shifted[slot, HALO + shifts[spin, column]]
            if best is not None:
                value = value * scale
                best = jnp.maximum(best, value)
            total[spin] = value
            return best

        return lax.fori_loop(0, spins, spindown, best, unroll=4)

    wait_edges(1, 0)
    forward(1)
    own.wait()
    wait_edges(0, 1)
    forward(0)
    wait_edges(3, 0)
    forward(3)
    wait_edges(2, 0)
    forward(2)
    load_shifts.wait()

    pairs = size // PAIR
    opens = 3 * pairs - 1
    wait_halo(0)
    wait_rest(1, PAIR - 1, local_segs, pair_recv.at[0])

    @pl.loop(0, 4 * pairs - 1)
    def _(turn):
        group = jnp.where(turn < 2 * pairs, turn // pairs, jnp.where(turn < opens, last_group, 5 - last_group))
        member = jnp.where(turn < opens, lax.rem(turn, pairs), turn - opens)
        pair = group * pairs + member

        @pl.when(jnp.logical_and(turn > 0, member == 0))
        def _():
            wait_halo(group)

        @pl.when(turn > 0)
        def _():
            wait_rest(PAIR, PAIR, local_segs, pair_recv.at[pair])

        @pl.loop(0, PAIR)
        def _(core):
            add([(pair * PAIR + core, seg) for seg in range(local_segs)])

    if pairs == 1:
        wait_halo(last_group)

    def lines_of(place):
        return [(last + core, begins[place] + seg) for core in range(PAIR) for seg in range(parts[place])]

    best = jnp.full((rows, bins), -jnp.inf, jnp.float32)
    for place, segs in enumerate(parts):
        wait_rest(PAIR, PAIR, segs, part_sem(last // PAIR, place))
        final = add(lines_of(place), best if place == len(parts) - 1 else None)
    best = final
    top = best[:, :EDGE]
    for begin in range(EDGE, bins, EDGE):
        top = jnp.maximum(top, best[:, begin : begin + EDGE])
    tops[0] = top

    def tell(step):
        return pltpu.make_async_remote_copy(
            src_ref=tops.at[0],
            dst_ref=tops.at[step],
            send_sem=top_send.at[step - 1],
            recv_sem=top_recv.at[step - 1],
            device_id={"seg": me, "freq": lax.rem(band + step, nfreq)},
            device_id_type=MESH,
        )

    for step in range(1, nfreq):
        tell(step).start()

    sent = coarse.at[:, pl.ds(0, (nseg - 1) * rows), :]
    wait_for(sent, send_sem)

    @pl.when(band < nfreq - 1)
    def _():
        wait_for(low, halo_send.at[0])

    @pl.when(band > 0)
    def _():
        wait_for(high, halo_send.at[halo_send.shape[0] - 1])

    for step in range(1, nfreq):
        tell(step).wait()
    top = tops[0]
    for step in range(1, nfreq):
        top = jnp.maximum(top, tops[step])
    total[spins, :, :EDGE] = top


def finish(total, fine, peaks, line, sem, line_sem):
    spins, rows = fine.shape[:2]
    write = pltpu.make_async_copy(total.at[pl.ds(0, spins)], fine, sem)
    write.start()
    row = lax.broadcasted_iota(jnp.int32, (rows, EDGE), 0)
    lane = lax.broadcasted_iota(jnp.int32, (rows, EDGE), 1)
    top = jnp.max(total[spins, :, :EDGE], axis=1, keepdims=True)
    line[...] = jnp.sum(jnp.where(row == lane, top, 0.0), axis=0)[:rows]
    write_line = pltpu.make_async_copy(line, peaks, line_sem)
    write_line.start()
    write.wait()
    write_line.wait()


def solution(mesh):
    nseg, nfreq = mesh.shape["seg"], mesh.shape["freq"]

    def on_device(coarse, offsets):
        local_segs, points, bins = coarse.shape
        rows = points // nseg
        spins = offsets.shape[1]
        parts = (local_segs - 2, 1, 1) if local_segs > 2 else (local_segs,)
        ways = 1 if nfreq <= 2 else 2
        hbm = pl.BlockSpec(memory_space=pltpu.HBM)
        vmem = pl.BlockSpec(memory_space=pltpu.VMEM)
        dma = pltpu.SemaphoreType.DMA
        signal = pltpu.SemaphoreType.REGULAR
        total = pl.pallas_call(
            functools.partial(kernel, nseg, nfreq, parts),
            out_shape=jax.ShapeDtypeStruct((spins + 1, rows, bins), jnp.float32),
            in_specs=[hbm, hbm],
            out_specs=vmem,
            scratch_shapes=[
                pltpu.VMEM((nseg, local_segs, rows, bins), jnp.float32),
                pltpu.VMEM((nseg, local_segs, rows, EDGE), jnp.float32),
                pltpu.VMEM((nseg, local_segs, rows, EDGE), jnp.float32),
                pltpu.VMEM((local_segs, SHIFTS, rows, bins), jnp.float32),
                pltpu.VMEM((nfreq, rows, EDGE), jnp.float32),
                pltpu.SMEM(offsets.shape[::-1], jnp.int32),
                dma,
                dma,
                dma,
                dma((PLANES,)),
                dma((nseg // PAIR,)),
                dma((max(len(parts) - 1, 1),)),
                dma((ways,)),
                dma((ways, PLANES)),
                dma((max(nfreq - 1, 1),)),
                dma((max(nfreq - 1, 1),)),
                signal,
                signal,
                signal,
            ],
            compiler_params=pltpu.CompilerParams(
                collective_id=0, has_side_effects=True, vmem_limit_bytes=32 << 20
            ),
        )(pltpu.with_memory_space_constraint(coarse, pltpu.HBM), pltpu.with_memory_space_constraint(offsets.T, pltpu.HBM))
        return pl.pallas_call(
            finish,
            out_shape=(
                jax.ShapeDtypeStruct((spins, rows, bins), jnp.float32),
                jax.ShapeDtypeStruct((rows,), jnp.float32),
            ),
            in_specs=[vmem],
            out_specs=(hbm, hbm),
            scratch_shapes=[pltpu.VMEM((rows,), jnp.float32), dma, dma],
            compiler_params=pltpu.CompilerParams(vmem_limit_bytes=8 << 20),
        )(total)

    return jax.shard_map(
        on_device,
        mesh=mesh,
        in_specs=(P("seg", None, "freq"), P()),
        out_specs=(P(None, "seg", "freq"), P("seg")),
        check_vma=False,
    )
```

time: 63.6 us -> 54.6 us (0.86)
  the two profiles are of different devices: /device:TPU:0 before, /device:TPU:8 now
where the time goes in v2:
time: 54.6 us; the launch traced here: 54.4 us
  Pallas kernels  53.8 us (99%)
  between operations  0.64 us (1%)
    pallas_call x1, Pallas kernels, on_device(): pl.pallas_call(functools.partial(kernel, nseg, nfreq, parts), out_shape=j...  52.8 us

profile of v2, /device:TPU:8, one launch (start us, length us, event | category | flops | bytes accessed | tf_op | source)
XLA Modules:
  0.0 54.4 jit_solution(6929084873152700838)
XLA Ops:
  0.6 52.8 %shard_map.41.total = f32[33,8,1024]{2,1,0:T(8,128)S(1)} custom-call(f32[4,128,1024]{2,1,0:T(8,128)} %coarse.1, s32[32,64]{1,0:T(8,128)} %bitcast.1), custom_call_target="tpu_custom_call" | custom-call | tf_op jit(solution)/shard_map/pallas_call | solution.py:375
  53.4 1.0 %shard_map.42 = (f32[32,8,1024]{2,1,0:T(8,128)}, f32[8]{0:T(128)}) custom-call(f32[33,8,1024]{2,1,0:T(8,128)S(1)} %shard_map.41.total), custom_call_target="tpu_custom_call" | custom-call | tf_op jit(solution)/shard_map/pallas_call | solution.py:405

commit v3 on v2

--- a/solution.py
+++ b/solution.py
@@ -12,6 +12,16 @@
 SHIFTS = 2 * HALO + 1
 PLANES = 4
 PAIR = 2
+ORDER = (
+    ("part", 0, 0),
+    ("part", 0, 1),
+    ("part", 1, 0),
+    ("part", 1, 1),
+    ("part", 2, 0),
+    ("part", 2, 1),
+    ("tail", 0),
+    ("tail", 1),
+)
 MESH = pl.DeviceIdType.MESH
 
 
@@ -45,6 +55,7 @@
     edge_recv,
     pair_recv,
     part_recv,
+    tail_recv,
     halo_send,
     halo_recv,
     top_send,
@@ -59,6 +70,7 @@
     scale = 1.0 / (nseg * local_segs)
     size = nseg // PLANES
     begins = [sum(parts[:place]) for place in range(len(parts))]
+    bulk = local_segs - 1
     me = lax.axis_index("seg")
     band = lax.axis_index("freq")
     plane = me // size
@@ -112,14 +124,25 @@
     def part_sem(pair, place):
         return part_recv.at[place - 1] if place else pair_recv.at[pair]
 
-    def send_parts(group):
-        core = lax.rem(me, PAIR)
+    def send_bulk(step):
+        if width:
+            send(step, rest_at, width, 0, bulk, pair_recv.at[step // PAIR])
+
+    def send_ends(group):
         first = (group + 1) * size - PAIR
+        lead = group * size
+
+        def part(place, core):
+            step = first + lax.rem(lax.rem(me, PAIR) + core, PAIR)
+            send(step, rest_at, width, begins[place], parts[place], part_sem(first // PAIR, place))
+
+        def tail(core):
+            step = lead + lax.rem(lax.rem(me, PAIR) + core, PAIR)
+            send(step, rest_at, width, bulk, 1, tail_recv)
+
         if width:
-            for place, segs in enumerate(parts):
-                for turn in range(PAIR):
-                    step = first + lax.rem(core + turn, PAIR)
-                    send(step, rest_at, width, begins[place], segs, part_sem(first // PAIR, place))
+            for act, *args in ORDER:
+                (part if act == "part" else tail)(*args)
 
     def wait_for(there, sem):
         pltpu.make_async_copy(there, there, sem).wait()
@@ -184,7 +207,7 @@
         for step in range(3 * size, 3 * size + PAIR):
             send_edge(step)
         for step in range(3 * size, 3 * size + PAIR):
-            send_rest(step)
+            send_bulk(step)
 
     @pl.when(outer)
     def _():
@@ -215,17 +238,18 @@
     def _():
         pl.semaphore_wait(near_sem, size)
         greet(3 * size, far_sem)
-        each(size, 2 * size, send_edge)
-        each(1, size, send_edge)
-        each(1, 2 * size, send_rest)
         pl.semaphore_wait(far_sem, 1)
         greet(size, near_sem)
         each(3 * size + PAIR, nseg, send_edge)
         each(2 * size, 3 * size, send_edge)
-        each(2 * size, 3 * size - PAIR, send_rest)
-        send_parts(2)
+        each(size, 2 * size, send_edge)
+        each(1, size, send_edge)
+        each(1, 2 * size, send_rest)
+        each(2 * size, 2 * size + PAIR, send_bulk)
+        each(2 * size + PAIR, 3 * size - PAIR, send_rest)
+        send_ends(2)
         each(3 * size + PAIR, 4 * size - PAIR, send_rest)
-        send_parts(3)
+        send_ends(3)
         if nfreq > 1:
             pl.semaphore_wait(band_sem, 1)
 
@@ -240,13 +264,19 @@
         each(1, size, send_rest)
         each(size + PAIR, nseg, send_rest)
 
+    lane = lax.broadcasted_iota(jnp.int32, (rows, EDGE), 1)
+
+    def column_of(step, seg):
+        return partner(me, step, nseg) * local_segs + seg
+
+    def line_of(step, seg):
+        ring = jnp.where(lane < EDGE // 2, high[step, seg], low[step, seg])
+        return jnp.concatenate([maps[step, seg], ring], axis=1)
+
     def add(lines, best=None):
-        lane = lax.broadcasted_iota(jnp.int32, (rows, EDGE), 1)
-        columns = []
+        columns = [column_of(step, seg) for step, seg in lines]
         for slot, (step, seg) in enumerate(lines):
-            columns.append(partner(me, step, nseg) * local_segs + seg)
-            ring = jnp.where(lane < EDGE // 2, high[step, seg], low[step, seg])
-            line = jnp.concatenate([maps[step, seg], ring], axis=1)
+            line = line_of(step, seg)
             for shift in range(-HALO, HALO + 1):
                 turned = line if shift == 0 else pltpu.roll(line, (-shift) % (bins + EDGE), 1)
                 shifted[slot, HALO + shift] = turned[:, :bins]
@@ -261,7 +291,7 @@
             total[spin] = value
             return best
 
-        return lax.fori_loop(0, spins, spindown, best, unroll=4)
+        return lax.fori_loop(0, spins, spindown, best, unroll=4 if len(lines) > PAIR else 8)
 
     wait_edges(1, 0)
     forward(1)
@@ -289,25 +319,33 @@
         def _():
             wait_halo(group)
 
-        @pl.when(turn > 0)
-        def _():
-            wait_rest(PAIR, PAIR, local_segs, pair_recv.at[pair])
-
-        @pl.loop(0, PAIR)
-        def _(core):
-            add([(pair * PAIR + core, seg) for seg in range(local_segs)])
-
-    if pairs == 1:
-        wait_halo(last_group)
+        def take(segs, waits):
+            @pl.when(waits)
+            def _():
+                wait_rest(PAIR, PAIR, segs, pair_recv.at[pair])
+
+            @pl.loop(0, PAIR)
+            def _(core):
+                add([(pair * PAIR + core, seg) for seg in range(segs)])
+
+        @pl.when(turn != 2 * pairs)
+        def _():
+            take(local_segs, turn > 0)
+
+        @pl.when(turn == 2 * pairs)
+        def _():
+            take(bulk, True)
 
     def lines_of(place):
         return [(last + core, begins[place] + seg) for core in range(PAIR) for seg in range(parts[place])]
 
-    best = jnp.full((rows, bins), -jnp.inf, jnp.float32)
     for place, segs in enumerate(parts):
         wait_rest(PAIR, PAIR, segs, part_sem(last // PAIR, place))
-        final = add(lines_of(place), best if place == len(parts) - 1 else None)
-    best = final
+        add(lines_of(place))
+    wait_rest(PAIR, PAIR, 1, tail_recv)
+    best = add(
+        [(last_group * size + core, bulk) for core in range(PAIR)], jnp.full((rows, bins), -jnp.inf, jnp.float32)
+    )
     top = best[:, :EDGE]
     for begin in range(EDGE, bins, EDGE):
         top = jnp.maximum(top, best[:, begin : begin + EDGE])
@@ -366,7 +404,7 @@
         local_segs, points, bins = coarse.shape
         rows = points // nseg
         spins = offsets.shape[1]
-        parts = (local_segs - 2, 1, 1) if local_segs > 2 else (local_segs,)
+        parts = (local_segs - 2, 1, 1)
         ways = 1 if nfreq <= 2 else 2
         hbm = pl.BlockSpec(memory_space=pltpu.HBM)
         vmem = pl.BlockSpec(memory_space=pltpu.VMEM)
@@ -389,7 +427,8 @@
                 dma,
                 dma((PLANES,)),
                 dma((nseg // PAIR,)),
-                dma((max(len(parts) - 1, 1),)),
+                dma((len(parts) - 1,)),
+                dma,
                 dma((ways,)),
                 dma((ways, PLANES)),
                 dma((max(nfreq - 1, 1),)),

time: 54.6 us -> 54.1 us (level)
  no operation moved by 1% of the time
where the time goes in v3:
time: 54.1 us; the launch traced here: 54 us
  Pallas kernels  53.3 us (99%)
  between operations  0.64 us (1%)
    pallas_call x1, Pallas kernels, on_device(): pl.pallas_call(functools.partial(kernel, nseg, nfreq, parts), out_shape=j...  52.4 us

profile of v3, /device:TPU:8, one launch (start us, length us, event | category | flops | bytes accessed | tf_op | source)
XLA Modules:
  0.0 54.0 jit_solution(14261377328563339722)
XLA Ops:
  0.6 52.4 %shard_map.41.total = f32[33,8,1024]{2,1,0:T(8,128)S(1)} custom-call(f32[4,128,1024]{2,1,0:T(8,128)} %coarse.1, s32[32,64]{1,0:T(8,128)} %bitcast.1), custom_call_target="tpu_custom_call" | custom-call | tf_op jit(solution)/shard_map/pallas_call | solution.py:413
  53.0 1.0 %shard_map.42 = (f32[32,8,1024]{2,1,0:T(8,128)}, f32[8]{0:T(128)}) custom-call(f32[33,8,1024]{2,1,0:T(8,128)S(1)} %shard_map.41.total), custom_call_target="tpu_custom_call" | custom-call | tf_op jit(solution)/shard_map/pallas_call | solution.py:444

commit v4 on v3

--- a/solution.py
+++ b/solution.py
@@ -16,12 +16,13 @@
     ("part", 0, 0),
     ("part", 0, 1),
     ("part", 1, 0),
+    ("part", 2, 0),
     ("part", 1, 1),
-    ("part", 2, 0),
     ("part", 2, 1),
     ("tail", 0),
     ("tail", 1),
 )
+CHUNK = EDGE // 2
 MESH = pl.DeviceIdType.MESH
 
 
@@ -47,6 +48,8 @@
     low,
     high,
     shifted,
+    turned,
+    chunks,
     tops,
     shifts,
     own_sem,
@@ -269,29 +272,77 @@
     def column_of(step, seg):
         return partner(me, step, nseg) * local_segs + seg
 
-    def line_of(step, seg):
-        ring = jnp.where(lane < EDGE // 2, high[step, seg], low[step, seg])
-        return jnp.concatenate([maps[step, seg], ring], axis=1)
-
-    def add(lines, best=None):
+    def ring_of(step, seg):
+        return jnp.where(lane < EDGE // 2, high[step, seg], low[step, seg])
+
+    def add(lines):
         columns = [column_of(step, seg) for step, seg in lines]
         for slot, (step, seg) in enumerate(lines):
-            line = line_of(step, seg)
+            line = jnp.concatenate([maps[step, seg], ring_of(step, seg)], axis=1)
             for shift in range(-HALO, HALO + 1):
-                turned = line if shift == 0 else pltpu.roll(line, (-shift) % (bins + EDGE), 1)
-                shifted[slot, HALO + shift] = turned[:, :bins]
-
-        def spindown(spin, best):
+                turned_line = line if shift == 0 else pltpu.roll(line, (-shift) % (bins + EDGE), 1)
+                shifted[slot, HALO + shift] = turned_line[:, :bins]
+
+        @pl.loop(0, spins, unroll=4)
+        def _(spin):
             value = total[spin]
             for slot, column in enumerate(columns):
                 value = value + shifted[slot, HALO + shifts[spin, column]]
+            total[spin] = value
+
+    tiles = bins // EDGE
+    first_half = lane < CHUNK
+
+    def turn_totals():
+        @pl.loop(0, spins // 2, unroll=8)
+        def _(pair):
+            blocks = []
+            for at in range(0, bins, EDGE):
+                one = total[2 * pair, :, at : at + EDGE]
+                two = total[2 * pair + 1, :, at : at + EDGE]
+                blocks.append(jnp.where(first_half, one, pltpu.roll(two, CHUNK, 1)))
+                blocks.append(jnp.where(first_half, pltpu.roll(one, CHUNK, 1), two))
+            square = jnp.concatenate(blocks, axis=0).T
+            turned[2 * pair] = square[:CHUNK]
+            turned[2 * pair + 1] = square[CHUNK:]
+
+    def turn_back():
+        @pl.loop(0, spins // 2, unroll=8)
+        def _(pair):
+            square = jnp.concatenate([turned[2 * pair], turned[2 * pair + 1]], axis=0).T
+            for tile in range(tiles):
+                at = tile * EDGE
+                even = square[2 * tile * rows : (2 * tile + 1) * rows]
+                odd = square[(2 * tile + 1) * rows : (2 * tile + 2) * rows]
+                total[2 * pair, :, at : at + EDGE] = jnp.where(first_half, even, pltpu.roll(odd, CHUNK, 1))
+                total[2 * pair + 1, :, at : at + EDGE] = jnp.where(first_half, pltpu.roll(even, CHUNK, 1), odd)
+
+    def add_turned(lines, best=None):
+        columns = [column_of(step, seg) for step, seg in lines]
+        own_half = lane < CHUNK + CHUNK // 2
+        next_part = jnp.logical_and(lane >= CHUNK, own_half)
+        for slot, (step, seg) in enumerate(lines):
+            whole = [maps[step, seg, :, at : at + EDGE] for at in range(0, bins, EDGE)] + [ring_of(step, seg)]
+            half = [pltpu.roll(tile, CHUNK, 1) for tile in whole]
+            blocks = []
+            for tile in range(tiles):
+                blocks.append(jnp.where(own_half, whole[tile], whole[tile - 1]))
+                blocks.append(jnp.where(next_part, half[tile + 1], half[tile]))
+            square = jnp.concatenate(blocks, axis=0).T
+            chunks[slot, :HALO] = square[EDGE - HALO :]
+            chunks[slot, HALO:] = square[: CHUNK + HALO]
+
+        def spindown(spin, best):
+            value = turned[spin]
+            for slot, column in enumerate(columns):
+                value = value + chunks[slot, pl.ds(HALO + shifts[spin, column], CHUNK)]
             if best is not None:
                 value = value * scale
                 best = jnp.maximum(best, value)
-            total[spin] = value
+            turned[spin] = value
             return best
 
-        return lax.fori_loop(0, spins, spindown, best, unroll=4 if len(lines) > PAIR else 8)
+        return lax.fori_loop(0, spins, spindown, best, unroll=8)
 
     wait_edges(1, 0)
     forward(1)
@@ -339,16 +390,17 @@
     def lines_of(place):
         return [(last + core, begins[place] + seg) for core in range(PAIR) for seg in range(parts[place])]
 
+    turn_totals()
     for place, segs in enumerate(parts):
         wait_rest(PAIR, PAIR, segs, part_sem(last // PAIR, place))
-        add(lines_of(place))
+        add_turned(lines_of(place))
     wait_rest(PAIR, PAIR, 1, tail_recv)
-    best = add(
-        [(last_group * size + core, bulk) for core in range(PAIR)], jnp.full((rows, bins), -jnp.inf, jnp.float32)
+    best = add_turned(
+        [(last_group * size + core, bulk) for core in range(PAIR)], jnp.full((CHUNK, EDGE), -jnp.inf, jnp.float32)
     )
-    top = best[:, :EDGE]
-    for begin in range(EDGE, bins, EDGE):
-        top = jnp.maximum(top, best[:, begin : begin + EDGE])
+    top = best[:rows]
+    for begin in range(rows, CHUNK, rows):
+        top = jnp.maximum(top, best[begin : begin + rows])
     tops[0] = top
 
     def tell(step):
@@ -364,6 +416,7 @@
     for step in range(1, nfreq):
         tell(step).start()
 
+    turn_back()
     sent = coarse.at[:, pl.ds(0, (nseg - 1) * rows), :]
     wait_for(sent, send_sem)
 
@@ -387,10 +440,12 @@
     spins, rows = fine.shape[:2]
     write = pltpu.make_async_copy(total.at[pl.ds(0, spins)], fine, sem)
     write.start()
-    row = lax.broadcasted_iota(jnp.int32, (rows, EDGE), 0)
-    lane = lax.broadcasted_iota(jnp.int32, (rows, EDGE), 1)
-    top = jnp.max(total[spins, :, :EDGE], axis=1, keepdims=True)
-    line[...] = jnp.sum(jnp.where(row == lane, top, 0.0), axis=0)[:rows]
+    top = jnp.max(total[spins, :, :EDGE], axis=0, keepdims=True)
+    apart = EDGE // 2
+    while apart >= rows:
+        top = jnp.maximum(top, pltpu.roll(top, apart, 1))
+        apart //= 2
+    line[...] = top[0, :rows]
     write_line = pltpu.make_async_copy(line, peaks, line_sem)
     write_line.start()
     write.wait()
@@ -406,6 +461,8 @@
         spins = offsets.shape[1]
         parts = (local_segs - 2, 1, 1)
         ways = 1 if nfreq <= 2 else 2
+        if rows * bins != EDGE * CHUNK or nseg % (2 * PAIR * PLANES) or spins % 2:
+            raise ValueError("unsupported shape")
         hbm = pl.BlockSpec(memory_space=pltpu.HBM)
         vmem = pl.BlockSpec(memory_space=pltpu.VMEM)
         dma = pltpu.SemaphoreType.DMA
@@ -420,6 +477,8 @@
                 pltpu.VMEM((nseg, local_segs, rows, EDGE), jnp.float32),
                 pltpu.VMEM((nseg, local_segs, rows, EDGE), jnp.float32),
                 pltpu.VMEM((local_segs, SHIFTS, rows, bins), jnp.float32),
+                pltpu.VMEM((spins, CHUNK, EDGE), jnp.float32),
+                pltpu.VMEM((PAIR * max(parts), CHUNK + 2 * HALO, EDGE), jnp.float32),
                 pltpu.VMEM((nfreq, rows, EDGE), jnp.float32),
                 pltpu.SMEM(offsets.shape[::-1], jnp.int32),
                 dma,

time: 54.1 us -> 53.8 us (level)
  Pallas kernels: 53.3 us -> 52.7 us
    pallas_call x1, Pallas kernels: 52.4 us -> 51.7 us  [on_device(): pl.pallas_call(functools.partial(kernel, nseg, nfreq, parts), out_shape=j...]
where the time goes in v4:
time: 53.8 us; the launch traced here: 53.3 us
  Pallas kernels  52.7 us (98%)
  between operations  0.64 us (1%)
    pallas_call x1, Pallas kernels, on_device(): pl.pallas_call(functools.partial(kernel, nseg, nfreq, parts), out_shape=j...  51.7 us

profile of v4, /device:TPU:8, one launch (start us, length us, event | category | flops | bytes accessed | tf_op | source)
XLA Modules:
  0.0 53.3 jit_solution(13686151982618051347)
XLA Ops:
  0.6 51.7 %shard_map.41.total = f32[33,8,1024]{2,1,0:T(8,128)S(1)} custom-call(f32[4,128,1024]{2,1,0:T(8,128)} %coarse.1, s32[32,64]{1,0:T(8,128)} %bitcast.1), custom_call_target="tpu_custom_call" | custom-call | tf_op jit(solution)/shard_map/pallas_call | solution.py:470
  52.3 1.0 %shard_map.42 = (f32[32,8,1024]{2,1,0:T(8,128)}, f32[8]{0:T(128)}) custom-call(f32[33,8,1024]{2,1,0:T(8,128)S(1)} %shard_map.41.total), custom_call_target="tpu_custom_call" | custom-call | tf_op jit(solution)/shard_map/pallas_call | solution.py:503
